TPU v7x, 32 devices: a whole 2x2x4 slice. The times are simulated.
32 devices in a mesh: dp: 8 (over z, y), mp: 4 (over x, core).
Axes of the slice: x: 2, y: 2, z: 4, core: 2. Of those that a mesh axis runs over, the one named last changes fastest.
Arguments:
- noise_blocks: bfloat16 [64, 12800], P('dp'), may hold values from -6 to 6
- data_blocks: bfloat16 [64, 12800], P('dp'), may hold values from -6 to 6
- destination: int32 [64], replicated, may hold values from 0 to 63, as said below
- utt_blocks: int32 [8, 4], P('dp'), may hold values from 1 to 4, 8 in all within a row
- span_start: int32 [8, 4], P('dp'), may hold values from 0 to 19
- span_size: int32 [8, 4], P('dp'), may hold values from 44 to 64
- timestep: int32 [8, 4], P('dp'), may hold values from 1 to 63
- in_weight: bfloat16 [200, 1024], replicated, may hold values from -0.4375 to 0.4375
- norm_gain: bfloat16 [1024], replicated, may hold values from 0.5 to 1.5
- qkv_weight: bfloat16 [1024, 3, 512], P(None, None, 'mp'), may hold values from -4 to 4
- out_proj: bfloat16 [512, 1024], P('mp'), may hold values from -0.25 to 0.25
- final_gain: bfloat16 [1024], replicated, may hold values from 0.25 to 1.75
- vel_weight: bfloat16 [1024, 100], replicated, may hold values from -0.1875 to 0.1875
Outputs:
- grad_qkv: float32 [1024, 3, 512], P('dp', None, 'mp')
- grad_out: float32 [512, 1024], P('mp', 'dp')
Inputs may be any that keep to these rules, and one draw needn't show every extreme that they name: `destination`: A permutation of the 64 bin positions; a device sends to each bin either none or exactly 1 of its blocks.
All inputs are finite; a program needn't handle non-finite values.
Results may differ from a plain program's by a relative error of at most 0.004.
Values may be sent and summed in bfloat16 or wider, within the bound.
A program may use at most 64 MiB of HBM per device.

v0:
```python
import jax
import jax.numpy as jnp
from jax import lax
from jax.sharding import PartitionSpec as P

HEAD_DIM = 64
BLOCK = 128


def frame_table(lengths, starts, sizes, steps, rows):
    ends = jnp.cumsum(lengths)
    frame = jnp.arange(rows, dtype=jnp.int32)
    block_index = frame // BLOCK
    segment = jnp.sum((block_index[:, None] >= ends[None, :]).astype(jnp.int32), axis=1)
    member = segment[:, None] == jnp.arange(lengths.shape[0], dtype=jnp.int32)[None, :]
    first = jnp.sum(jnp.where(member, (ends - lengths)[None, :], 0), axis=1) * BLOCK
    span = jnp.sum(jnp.where(member, lengths[None, :], 0), axis=1) * BLOCK
    lower = jnp.sum(jnp.where(member, starts[None, :], 0), axis=1)
    upper = lower + jnp.sum(jnp.where(member, sizes[None, :], 0), axis=1)
    inside = 64 * (frame - first)
    masked = ((inside >= lower * span) & (inside < upper * span)).astype(jnp.float32)
    level = jnp.sum(jnp.where(member, steps[None, :], 0), axis=1).astype(jnp.float32) / 64.0
    return (segment, masked, level)


def attend(query, keys, values, segment):
    rows, width = query.shape
    heads = width // HEAD_DIM
    block = min(512, rows)
    reach = min(4, rows // BLOCK // 2) * BLOCK
    window = min(rows, block + 2 * reach)
    blocks = rows // block
    query_blocks = query.reshape(blocks, block, heads, HEAD_DIM)
    segment_blocks = segment.reshape(blocks, block)
    firsts = jnp.clip(jnp.arange(blocks, dtype=jnp.int32) * block - reach, 0, rows - window)
    keyed = keys.reshape(rows, heads, HEAD_DIM)
    valued = values.reshape(rows, heads, HEAD_DIM)

    def one_block(item):
        query_block, segment_block, first = item
        scores = jnp.einsum(
            "qhd,khd->hqk", query_block, keyed, preferred_element_type=jnp.float32
        ) * HEAD_DIM ** (-0.5)
        scores = jnp.where((segment_block[:, None] == segment[None, :])[None], scores, -1e30)
        top = jnp.max(scores, axis=-1, keepdims=True)
        weights = jnp.exp(scores - top)
        probs = (weights / jnp.sum(weights, axis=-1, keepdims=True)).astype(jnp.bfloat16)
        return jnp.einsum(
            "hqk,khd->qhd", probs, valued, preferred_element_type=jnp.float32
        ).reshape(block, width)

    return lax.map(jax.checkpoint(one_block), (query_blocks, segment_blocks, firsts)).reshape(
        rows, width
    )


def shards(
    noise_blocks,
    data_blocks,
    destination,
    utt_blocks,
    span_start,
    span_size,
    timestep,
    in_weight,
    norm_gain,
    qkv_weight,
    out_proj,
    final_gain,
    vel_weight,
):
    sources = lax.axis_size("dp")
    here = lax.axis_index("dp")
    per_dev = noise_blocks.shape[0]
    depth = max(1, per_dev // sources)
    lanes_total = sources * depth
    table = destination.reshape(sources, per_dev)
    owner = table // per_dev
    order = jnp.arange(per_dev, dtype=jnp.int32)
    earlier = (owner[:, :, None] == owner[:, None, :]) & (
        order[None, None, :] < order[None, :, None]
    )
    rank = jnp.sum(earlier.astype(jnp.int32), axis=2)
    code = jnp.arange(sources, dtype=jnp.int32)[:, None] * depth + rank
    mine_owner = lax.dynamic_index_in_dim(owner, here, 0, keepdims=False)
    mine_rank = lax.dynamic_index_in_dim(rank, here, 0, keepdims=False)
    lanes = jnp.arange(lanes_total, dtype=jnp.int32)
    packing = (lanes[:, None] == (mine_owner * depth + mine_rank)[None, :]).astype(jnp.bfloat16)
    wanted = here * per_dev + order
    hit = table[None, :, :] == wanted[:, None, None]
    source_code = jnp.sum(jnp.where(hit, code[None, :, :], 0), axis=(1, 2))
    unpacking = (source_code[:, None] == lanes[None, :]).astype(jnp.bfloat16)

    def outgoing(blocks):
        sent = jnp.dot(packing, blocks, preferred_element_type=jnp.float32).astype(jnp.bfloat16)
        return sent.reshape(sources, depth, blocks.shape[1])

    def incoming(arrived):
        flat = arrived.reshape(lanes_total, arrived.shape[2])
        return jnp.dot(unpacking, flat, preferred_element_type=jnp.float32).astype(jnp.bfloat16)

    got_noise, got_data = (
        lax.all_to_all(outgoing(noise_blocks), "dp", split_axis=0, concat_axis=0, tiled=True),
        lax.all_to_all(outgoing(data_blocks), "dp", split_axis=0, concat_axis=0, tiled=True),
    )
    bin_noise = incoming(got_noise)
    bin_data = incoming(got_data)
    rows = per_dev * BLOCK
    mel = noise_blocks.shape[1] // BLOCK
    noise = bin_noise.reshape(rows, mel).astype(jnp.float32)
    data = bin_data.reshape(rows, mel).astype(jnp.float32)
    segment, masked, level = frame_table(
        utt_blocks[0], span_start[0], span_size[0], timestep[0], rows
    )
    noisy = (1.0 - level[:, None]) * noise + level[:, None] * data
    cond = data * (1.0 - masked[:, None])
    target = data - noise
    inputs = jnp.concatenate([noisy, cond], axis=1).astype(jnp.bfloat16)
    hidden0 = jnp.dot(inputs, in_weight, preferred_element_type=jnp.float32)
    scale = lax.rsqrt(jnp.mean(hidden0 * hidden0, axis=1, keepdims=True) + 1e-06)
    normed = (hidden0 * scale * norm_gain.astype(jnp.float32)[None, :]).astype(jnp.bfloat16)
    query = jnp.dot(normed, qkv_weight[:, 0, :], preferred_element_type=jnp.float32).astype(
        jnp.bfloat16
    )
    keys = jnp.dot(normed, qkv_weight[:, 1, :], preferred_element_type=jnp.float32).astype(
        jnp.bfloat16
    )
    values = jnp.dot(normed, qkv_weight[:, 2, :], preferred_element_type=jnp.float32).astype(
        jnp.bfloat16
    )
    heads_out, pullback = jax.vjp(lambda a, b, c: attend(a, b, c, segment), query, keys, values)
    attended = heads_out.astype(jnp.bfloat16)
    partial_mix = jnp.dot(attended, out_proj, preferred_element_type=jnp.float32)
    mixed = lax.psum(partial_mix.astype(jnp.bfloat16), "mp").astype(jnp.float32)
    hidden1 = (hidden0 + mixed).astype(jnp.bfloat16)
    wide1 = lax.optimization_barrier(hidden1).astype(jnp.float32)
    rscale = lax.rsqrt(jnp.mean(wide1 * wide1, axis=1, keepdims=True) + 1e-06)
    normalized = wide1 * rscale
    gain_out = final_gain.astype(jnp.float32)[None, :]
    final = (normalized * gain_out).astype(jnp.bfloat16)
    velocity = jnp.dot(final, vel_weight, preferred_element_type=jnp.float32)
    count = lax.psum(jnp.sum(masked), "dp")
    error = (2.0 * masked[:, None] * (velocity - target)).astype(jnp.bfloat16)
    grad_final = jnp.dot(error, vel_weight.T, preferred_element_type=jnp.float32)
    scaled = grad_final * gain_out
    back1 = (
        rscale * (scaled - normalized * jnp.mean(scaled * normalized, axis=1, keepdims=True))
    ).astype(jnp.bfloat16)
    back_att = jnp.dot(back1, out_proj.T, preferred_element_type=jnp.float32).astype(jnp.bfloat16)
    dquery, dkeys, dvalues = pullback(back_att.astype(jnp.float32))
    out_terms = jnp.dot(attended.T, back1, preferred_element_type=jnp.float32)
    qkv_terms = jnp.stack(
        [
            jnp.dot(normed.T, dquery, preferred_element_type=jnp.float32),
            jnp.dot(normed.T, dkeys, preferred_element_type=jnp.float32),
            jnp.dot(normed.T, dvalues, preferred_element_type=jnp.float32),
        ],
        axis=1,
    )
    summed_qkv, summed_out = (
        lax.psum_scatter(qkv_terms, "dp", scatter_dimension=0, tiled=True),
        lax.psum_scatter(out_terms, "dp", scatter_dimension=1, tiled=True),
    )
    return (summed_qkv / count, summed_out / count)


def solution(mesh):
    in_specs = (
        P("dp", None),
        P("dp", None),
        P(),
        P("dp", None),
        P("dp", None),
        P("dp", None),
        P("dp", None),
        P(),
        P(),
        P(None, None, "mp"),
        P("mp", None),
        P(),
        P(),
    )
    out_specs = (P("dp", None, "mp"), P("mp", "dp"))
    return jax.shard_map(shards, mesh=mesh, in_specs=in_specs, out_specs=out_specs, check_vma=False)
```

profile of v0, /device:TPU:0, one launch (start us, length us, event | category | flops | bytes accessed | tf_op | source)
XLA Modules:
  0.0 272.0 jit_solution(2920325727797531894)
XLA Ops:
  8.3 1.1 fusion.60
  11.4 7.3 %all-to-all-start = ((bf16[8,2,6400]{2,1,0:T(2,128)(2,1)}), bf16[8,2,6400]{2,1,0:T(2,128)(2,1)S(1)}, u32[]{:S(2)}, u32[]{:S(2)}) async-start(bf16[8,2,6400]{2,1,0:T(2,128)(2,1)} %reshape.344), calls=%async_computation | async-start | bytes 409600 | tf_op jit(solution)/shard_map/all_to_all | solution.py:103
  21.7 1.1 fusion.61
  24.4 2.4 all-to-all-done
  26.8 3.6 %all-to-all-start.1 = ((bf16[8,2,6400]{2,1,0:T(2,128)(2,1)}), bf16[8,2,6400]{2,1,0:T(2,128)(2,1)S(1)}, u32[]{:S(2)}, u32[]{:S(2)}) async-start(bf16[8,2,6400]{2,1,0:T(2,128)(2,1)} %reshape.342), calls=%async_computation.1 | async-start | bytes 409600 | tf_op jit(solution)/shard_map/all_to_all | solution.py:104
  33.4 4.8 %all-to-all-done.1 = bf16[8,2,6400]{2,1,0:T(2,128)(2,1)S(1)} async-done(((bf16[8,2,6400]{2,1,0:T(2,128)(2,1)}), bf16[8,2,6400]{2,1,0:T(2,128)(2,1)S(1)}, u32[]{:S(2)}, u32[]{:S(2)}) %all-to-all-start.1) | async-done | bytes 204832 | tf_op jit(solution)/shard_map/all_to_all | solution.py:104
  41.4 1.3 copy-done.16
  44.1 1.2 convolution_convert_fusion.7
  45.5 1.0 copy.56
  46.5 17.6 %while.30 = (s32[]{:T(128)}, bf16[2,512,128]{2,1,0:T(8,128)(2,1)S(1)}, s32[2,512]{1,0:T(2,128)}, s32[1,1024]{1,0:T(1,128)S(1)}, bf16[2,512,2,64]{1,3,2,0:T(8,128...) while((s32[]{:T(128)}, bf16[2,512,128]{2,1,0:T(8,128)(2,1)S(1)}, ...), condition=%wide.region_13.14_spmd, body=%wide.region_10.13_spmd.sunk | while | flops 275252224 | bytes 11815545 | solution.py:52
  47.6 4.5 %fusion.178 = (f32[2,512]{1,0:T(2,128)S(1)}, f32[2,512,1024]{2,1,0:T(8,128)}) fusion(pred[512,1024]{1,0:T(8,128)(4,1)S(1)} %broadcast_compare_fusion.4, bf16[1024,2,64]{0,2,1:T(8,128)(2,1)S(1)} %get-tuple-element.617, bf16[2,512,2,64]{1,3,2,0:T(8,128)(2,1)} %get-tuple-element.616, s32[]{:T(128)} %get-tuple-element.604), kind=kOutput, calls=%fused_computation.176.clone.1 | convolution fusion | flops 138413056 | bytes 5116416 | tf_op jit(solution)/shard_map/jvp()/while/body/eval_jaxpr/sub | solution.py:46
  52.2 3.0 %fusion.179 = bf16[2,512,64]{1,2,0:T(8,128)(2,1)S(1)} fusion(bf16[1024,2,64]{0,2,1:T(8,128)(2,1)S(1)} %copy-done.19, f32[2,512,1024]{2,1,0:T(8,128)} %get-tuple-element.570, f32[2,512]{1,0:T(2,128)S(1)} %get-tuple-element.571), kind=kOutput, calls=%fused_computation.8.clone.1 | convolution fusion | flops 136314880 | bytes 4591616 | tf_op jit(solution)/shard_map/jvp()/while/body/eval_jaxpr/hqk,khd->qhd/dot_general | solution.py:48
  56.4 4.5 %fusion.178 = (f32[2,512]{1,0:T(2,128)S(1)}, f32[2,512,1024]{2,1,0:T(8,128)}) fusion(pred[512,1024]{1,0:T(8,128)(4,1)S(1)} %broadcast_compare_fusion.4, bf16[1024,2,64]{0,2,1:T(8,128)(2,1)S(1)} %get-tuple-element.617, bf16[2,512,2,64]{1,3,2,0:T(8,128)(2,1)} %get-tuple-element.616, s32[]{:T(128)} %get-tuple-element.604), kind=kOutput, calls=%fused_computation.176.clone.1 | convolution fusion | flops 138413056 | bytes 5116416 | tf_op jit(solution)/shard_map/jvp()/while/body/eval_jaxpr/sub | solution.py:46
  60.9 3.0 %fusion.179 = bf16[2,512,64]{1,2,0:T(8,128)(2,1)S(1)} fusion(bf16[1024,2,64]{0,2,1:T(8,128)(2,1)S(1)} %copy-done.19, f32[2,512,1024]{2,1,0:T(8,128)} %get-tuple-element.570, f32[2,512]{1,0:T(2,128)S(1)} %get-tuple-element.571), kind=kOutput, calls=%fused_computation.8.clone.1 | convolution fusion | flops 136314880 | bytes 4591616 | tf_op jit(solution)/shard_map/jvp()/while/body/eval_jaxpr/hqk,khd->qhd/dot_general | solution.py:48
  64.2 2.1 convolution_convert_fusion.5
  66.8 1.0 copy.54
  67.8 48.4 %all-reduce.2.cloned.1.call-done = bf16[1024,1024]{0,1:T(8,128)(2,1)} async-done(((bf16[1024,1024]{0,1:T(8,128)(2,1)}), bf16[1024,1024]{0,1:T(8,128)(2,1)}) %all-reduce.2.cloned.1.call-update) | async-done | bytes 2097168 | tf_op jit(solution)/shard_map/psum | solution.py:134
  116.2 3.6 %add_convert_fusion = bf16[1024,1024]{0,1:T(8,128)(2,1)S(1)} fusion(f32[1024,1024]{0,1:T(8,128)} %copy-done.4, bf16[1024,1024]{0,1:T(8,128)(2,1)} %all-reduce.2.cloned.1.call-done), kind=kLoop, calls=%fused_computation.88 | loop fusion | flops 3145728 | bytes 8388608 | tf_op jit(solution)/shard_map/convert_element_type | solution.py:135
  120.3 4.7 %fusion.66 = (f32[1024]{0:T(1024)S(1)}, f32[1024,1024]{0,1:T(8,128)}) fusion(bf16[1024,1024]{0,1:T(8,128)(2,1)S(1)} %add_convert_fusion, f32[1024]{0:T(1024)S(1)} %convert_element_type.200, f32[1024]{0:T(1024)S(1)} %add_rsqrt_fusion, bf16[1024,100]{0,1:T(8,128)(2,1)} %param.29, f32[1024,100]{0,1:T(8,128)} %copy.54, f32[1024,100]{0,1:T(8,128)S(1)} %copy.55, ...), kind=kOutput, calls=%fused_computation.83 | convolution fusion | flops 429276160 | bytes 7331840 | tf_op jit(solution)/shard_map/dot_general | solution.py:144
  125.0 3.7 %fusion.69 = bf16[1024,1024]{0,1:T(8,128)(2,1)S(1)} fusion(bf16[1024,1024]{0,1:T(8,128)(2,1)} %copy-done.7, f32[1024,1024]{0,1:T(8,128)} %get-tuple-element.459, f32[1024]{0:T(1024)S(1)} %broadcast_multiply_fusion, f32[1024]{0:T(1024)S(1)} %convert_element_type.200, f32[1024]{0:T(1024)S(1)} %add_rsqrt_fusion), kind=kLoop, calls=%fused_computation.86 | loop fusion | flops 7340032 | bytes 8400896 | tf_op jit(solution)/shard_map/convert_element_type | solution.py:148
  128.8 1.6 fusion.126
  132.0 44.7 %while.31 = (s32[]{:T(128)}, bf16[1024,2,64]{0,2,1:T(8,128)(2,1)}, bf16[1024,2,64]{0,2,1:T(8,128)(2,1)}, bf16[2,512,2,64]{1,3,2,0:T(8,128)(2,1)}, bf16[2,512,2,6...) while((s32[]{:T(128)}, bf16[1024,2,64]{0,2,1:T(8,128)(2,1)}, ...), condition=%wide.region_23.24_spmd.clone, body=%wide.region_17.23_spmd.clone.sunk | while | flops 712179712 | bytes 109349352 | solution.py:52
  132.1 1.0 dynamic-slice_bitcast_fusion.2
  133.8 1.0 broadcast_compare_fusion.5
  134.9 2.1 fusion.187
  137.0 1.2 fusion.188
  138.2 2.8 %convert_reduce_fusion.5 = (f32[2,512]{1,0:T(2,128)S(1)}, pred[2,512,1024]{2,1,0:T(32,128)(4,1)S(1)}, f32[2,512]{1,0:T(2,128)S(1)}, bf16[2,512,1024]{2,1,0:T(8,128)(2,1)S(1)}) fusion(f32[2,512]{1,0:T(2,128)S(1)} %get-tuple-element.586, f32[2,512,1024]{2,1,0:T(8,128)S(1)} %get-tuple-element.587, pred[512,1024]{1,0:T(8,128)(4,1)S(1)} %broadcast_compare_fusion.5, ...), kind=kOutput, calls=%fused_computation.30.clone.1 | convolution fusion | flops 144701440 | bytes 8273920 | tf_op jit(solution)/shard_map/transpose(jvp())/while/body/eval_jaxpr/checkpoint/hqk,khd->qhd/dot_general | solution.py:48
  141.0 1.9 fusion.189
  143.0 1.9 copy-done.2
  144.9 2.2 fusion.192
  147.1 4.5 %fusion.191 = bf16[1024,2,64]{0,2,1:T(8,128)(2,1)} fusion(bf16[2,64,512]{2,1,0:T(8,128)(2,1)S(1)} %bitcast.163, f32[2,512]{1,0:T(2,128)} %copy-done.9, f32[2,512,1024]{2,1,0:T(8,128)} %copy-done.1, f32[2,512]{1,0:T(2,128)} %copy-done.11, pred[512,1024]{1,0:T(8,128)(4,1)S(1)} %broadcast_compare_fusion.5, ...), kind=kOutput, calls=%fused_computation.52.clone.1 | convolution fusion | flops 139722752 | bytes 5382145 | tf_op jit(solution)/shard_map/transpose(jvp())/while/body/eval_jaxpr/checkpoint/hqk,khd->qhd/dot_general | solution.py:48
  151.6 2.3 fusion.190
  155.6 1.0 broadcast_compare_fusion.5
  156.7 2.1 fusion.187
  158.8 1.2 fusion.188
  160.0 2.8 %convert_reduce_fusion.5 = (f32[2,512]{1,0:T(2,128)S(1)}, pred[2,512,1024]{2,1,0:T(32,128)(4,1)S(1)}, f32[2,512]{1,0:T(2,128)S(1)}, bf16[2,512,1024]{2,1,0:T(8,128)(2,1)S(1)}) fusion(f32[2,512]{1,0:T(2,128)S(1)} %get-tuple-element.586, f32[2,512,1024]{2,1,0:T(8,128)S(1)} %get-tuple-element.587, pred[512,1024]{1,0:T(8,128)(4,1)S(1)} %broadcast_compare_fusion.5, ...), kind=kOutput, calls=%fused_computation.30.clone.1 | convolution fusion | flops 144701440 | bytes 8273920 | tf_op jit(solution)/shard_map/transpose(jvp())/while/body/eval_jaxpr/checkpoint/hqk,khd->qhd/dot_general | solution.py:48
  162.9 1.9 fusion.189
  164.8 1.9 copy-done.2
  166.7 2.2 fusion.192
  168.9 4.6 %fusion.191 = bf16[1024,2,64]{0,2,1:T(8,128)(2,1)} fusion(bf16[2,64,512]{2,1,0:T(8,128)(2,1)S(1)} %bitcast.163, f32[2,512]{1,0:T(2,128)} %copy-done.9, f32[2,512,1024]{2,1,0:T(8,128)} %copy-done.1, f32[2,512]{1,0:T(2,128)} %copy-done.11, pred[512,1024]{1,0:T(8,128)(4,1)S(1)} %broadcast_compare_fusion.5, ...), kind=kOutput, calls=%fused_computation.52.clone.1 | convolution fusion | flops 139722752 | bytes 5382145 | tf_op jit(solution)/shard_map/transpose(jvp())/while/body/eval_jaxpr/checkpoint/hqk,khd->qhd/dot_general | solution.py:48
  173.5 3.2 %fusion.190 = bf16[1024,2,64]{0,2,1:T(8,128)(2,1)} fusion(bf16[512,2,64]{0,2,1:T(8,128)(2,1)S(1)} %dynamic-slice_bitcast_fusion.2, f32[2,512,1024]{2,1,0:T(8,128)S(1)} %copy-done.3, pred[2,512,1024]{2,1,0:T(32,128)(4,1)S(1)} %copy-done.22, f32[2,512]{1,0:T(2,128)S(1)} %copy-done.14, pred[512,1024]{1,0:T(8,128)(4,1)S(1)} %broadcast_compare_fusion.5, ...), kind=kOutput, calls=%fused_computation.53.clone.1 | convolution fusion | flops 138805248 | bytes 6426625 | tf_op jit(solution)/shard_map/transpose(jvp())/while/body/eval_jaxpr/checkpoint/qhd,khd->hqk/dot_general | solution.py:41
  176.7 1.3 copy.58
  178.7 1.7 convolution_bitcast_fusion.1
  181.1 1.3 pad_maximum_fusion
  182.4 21.8 %psum.15 = f32[]{:T(128)} all-reduce(f32[]{:T(128)} %get-tuple-element.442), channel_id=1, replica_groups=mesh['dp'=8,'mp'=4] {'dp'}, use_global_device_ids=true, to_apply=%region_26.27 | all-reduce | flops 1 | bytes 8 | tf_op jit(solution)/shard_map/psum | solution.py:142
  204.2 2.0 broadcast_divide_fusion.1
  206.2 57.0 %reduce-scatter.3.cloned.1.call-done = f32[128,3,128]{2,0,1:T(8,128)} async-done(((f32[1024,3,128]{2,0,1:T(8,128)}), f32[128,3,128]{2,0,1:T(8,128)}) %reduce-scatter.3.cloned.1.call-update) | async-done | bytes 196624 | tf_op jit(solution)/shard_map/reduce_scatter | solution.py:161
  263.3 2.2 broadcast_divide_fusion
  (144 shorter events, 24.4 us)
Async XLA Ops:
  7.2 32.9 %copy-start = (bf16[200,1024]{1,0:T(8,128)(2,1)S(1)}, bf16[200,1024]{1,0:T(8,128)(2,1)}, u32[]{:S(2)}) copy-start(bf16[200,1024]{1,0:T(8,128)(2,1)} %param.24) | copy-start | bytes 1228804
  11.4 15.4 %all-to-all-start = ((bf16[8,2,6400]{2,1,0:T(2,128)(2,1)}), bf16[8,2,6400]{2,1,0:T(2,128)(2,1)S(1)}, u32[]{:S(2)}, u32[]{:S(2)}) async-start(bf16[8,2,6400]{2,1,0:T(2,128)(2,1)} %reshape.344), calls=%async_computation | async-start | bytes 409600 | tf_op jit(solution)/shard_map/all_to_all | solution.py:103
  26.8 11.4 %all-to-all-start.1 = ((bf16[8,2,6400]{2,1,0:T(2,128)(2,1)}), bf16[8,2,6400]{2,1,0:T(2,128)(2,1)S(1)}, u32[]{:S(2)}, u32[]{:S(2)}) async-start(bf16[8,2,6400]{2,1,0:T(2,128)(2,1)} %reshape.342), calls=%async_computation.1 | async-start | bytes 409600 | tf_op jit(solution)/shard_map/all_to_all | solution.py:104
  30.4 85.8 %all-reduce.2.cloned.1.call-start = ((), (), s32[]{:S(2)}) async-start(), calls=%async_computation.4 | async-start | bytes 4194304 | tf_op jit(solution)/shard_map/psum | solution.py:134
  41.0 2.5 copy-start.4
  41.0 1.7 copy-start.16
  42.7 1.4 copy-start.5
  46.5 17.6 %copy-start.8 = (bf16[128,1024]{1,0:T(8,128)(2,1)S(1)}, bf16[128,1024]{1,0:T(8,128)(2,1)}, u32[]{:S(2)}) copy-start(bf16[128,1024]{1,0:T(8,128)(2,1)} %param.27) | copy-start | bytes 786436
  47.3 4.9 %copy-start.19 = (bf16[1024,2,64]{0,2,1:T(8,128)(2,1)S(1)}, bf16[1024,2,64]{0,2,1:T(8,128)(2,1)}, u32[]{:S(2)}) copy-start(bf16[1024,2,64]{0,2,1:T(8,128)(2,1)} %get-tuple-element.618) | copy-start | bytes 786436 | tf_op jit(solution)/shard_map/jvp()/while
  56.0 4.9 %copy-start.19 = (bf16[1024,2,64]{0,2,1:T(8,128)(2,1)S(1)}, bf16[1024,2,64]{0,2,1:T(8,128)(2,1)}, u32[]{:S(2)}) copy-start(bf16[1024,2,64]{0,2,1:T(8,128)(2,1)} %get-tuple-element.618) | copy-start | bytes 786436 | tf_op jit(solution)/shard_map/jvp()/while
  64.1 2.4 copy-start.17
  64.1 3.7 %copy-start.10 = (s32[1,1024]{1,0:T(1,128)}, s32[1,1024]{1,0:T(1,128)S(1)}, u32[]{:S(2)}) copy-start(s32[1,1024]{1,0:T(1,128)S(1)} %get-tuple-element.668) | copy-start | bytes 12292
  64.1 2.4 copy-start.15
  66.3 137.9 %reduce-scatter.5.cloned.1.call-start = ((), (), s32[]{:S(2)}) async-start(), calls=%async_computation.6 | async-start | bytes 589824 | tf_op jit(solution)/shard_map/reduce_scatter | solution.py:162
  119.8 5.2 %copy-start.7 = (bf16[1024,1024]{0,1:T(8,128)(2,1)}, bf16[1024,1024]{0,1:T(8,128)(2,1)S(1)}, u32[]{:S(2)}) copy-start(bf16[1024,1024]{0,1:T(8,128)(2,1)S(1)} %add_convert_fusion) | copy-start | bytes 6291460
  131.2 132.1 %reduce-scatter.3.cloned.1.call-start = ((), (), s32[]{:S(2)}) async-start(), calls=%async_computation.5 | async-start | bytes 1769472 | tf_op jit(solution)/shard_map/reduce_scatter | solution.py:161
  132.0 46.0 %copy-start.6 = (bf16[1024,1024]{0,1:T(8,128)(2,1)S(1)}, bf16[1024,1024]{0,1:T(8,128)(2,1)}, u32[]{:S(2)}) copy-start(bf16[1024,1024]{0,1:T(8,128)(2,1)} %copy-done.5) | copy-start | bytes 6291460
  134.9 3.3 %copy-start.20 = (bf16[1024,2,64]{0,2,1:T(8,128)(2,1)S(1)}, bf16[1024,2,64]{0,2,1:T(8,128)(2,1)}, u32[]{:S(2)}) copy-start(bf16[1024,2,64]{0,2,1:T(8,128)(2,1)} %get-tuple-element.589) | copy-start | bytes 786436 | tf_op jit(solution)/shard_map/transpose(jvp())/while
  137.0 4.0 %copy-start.1 = (f32[2,512,1024]{2,1,0:T(8,128)}, f32[2,512,1024]{2,1,0:T(8,128)S(1)}, u32[]{:S(2)}) copy-start(f32[2,512,1024]{2,1,0:T(8,128)S(1)} %get-tuple-element.587) | copy-start | bytes 12582916 | tf_op jit(solution)/shard_map/transpose(jvp())/while
  137.0 4.0 %copy-start.11 = (f32[2,512]{1,0:T(2,128)}, f32[2,512]{1,0:T(2,128)S(1)}, u32[]{:S(2)}) copy-start(f32[2,512]{1,0:T(2,128)S(1)} %get-tuple-element.586) | copy-start | bytes 12292 | tf_op jit(solution)/shard_map/transpose(jvp())/while
  138.2 2.9 %copy-start.9 = (f32[2,512]{1,0:T(2,128)}, f32[2,512]{1,0:T(2,128)S(1)}, u32[]{:S(2)}) copy-start(f32[2,512]{1,0:T(2,128)S(1)} %fusion.188) | copy-start | bytes 12292 | tf_op jit(solution)/shard_map/transpose(jvp())/while
  141.0 2.0 copy-start.21
  141.0 3.9 %copy-start.18 = (bf16[1024,2,64]{0,2,1:T(8,128)(2,1)S(1)}, bf16[1024,2,64]{0,2,1:T(8,128)(2,1)}, u32[]{:S(2)}) copy-start(bf16[1024,2,64]{0,2,1:T(8,128)(2,1)} %get-tuple-element.585) | copy-start | bytes 786436 | tf_op jit(solution)/shard_map/transpose(jvp())/while
  143.0 2.0 copy-start.2
  143.0 1.9 copy-start.13
  147.1 4.5 %copy-start.3 = (f32[2,512,1024]{2,1,0:T(8,128)S(1)}, f32[2,512,1024]{2,1,0:T(8,128)}, u32[]{:S(2)}) copy-start(f32[2,512,1024]{2,1,0:T(8,128)} %copy-done.2) | copy-start | bytes 12582916 | tf_op jit(solution)/shard_map/transpose(jvp())/while
  147.1 4.5 %copy-start.14 = (f32[2,512]{1,0:T(2,128)S(1)}, f32[2,512]{1,0:T(2,128)}, u32[]{:S(2)}) copy-start(f32[2,512]{1,0:T(2,128)} %copy-done.13) | copy-start | bytes 12292 | tf_op jit(solution)/shard_map/transpose(jvp())/while
  147.1 4.5 %copy-start.22 = (pred[2,512,1024]{2,1,0:T(32,128)(4,1)S(1)}, pred[2,512,1024]{2,1,0:T(32,128)(4,1)}, u32[]{:S(2)}) copy-start(pred[2,512,1024]{2,1,0:T(32,128)(4,1)} %copy-done.21) | copy-start | bytes 3145732 | tf_op jit(solution)/shard_map/transpose(jvp())/while
  156.7 3.3 %copy-start.20 = (bf16[1024,2,64]{0,2,1:T(8,128)(2,1)S(1)}, bf16[1024,2,64]{0,2,1:T(8,128)(2,1)}, u32[]{:S(2)}) copy-start(bf16[1024,2,64]{0,2,1:T(8,128)(2,1)} %get-tuple-element.589) | copy-start | bytes 786436 | tf_op jit(solution)/shard_map/transpose(jvp())/while
  158.8 4.0 %copy-start.1 = (f32[2,512,1024]{2,1,0:T(8,128)}, f32[2,512,1024]{2,1,0:T(8,128)S(1)}, u32[]{:S(2)}) copy-start(f32[2,512,1024]{2,1,0:T(8,128)S(1)} %get-tuple-element.587) | copy-start | bytes 12582916 | tf_op jit(solution)/shard_map/transpose(jvp())/while
  158.8 4.0 %copy-start.11 = (f32[2,512]{1,0:T(2,128)}, f32[2,512]{1,0:T(2,128)S(1)}, u32[]{:S(2)}) copy-start(f32[2,512]{1,0:T(2,128)S(1)} %get-tuple-element.586) | copy-start | bytes 12292 | tf_op jit(solution)/shard_map/transpose(jvp())/while
  160.0 2.9 %copy-start.9 = (f32[2,512]{1,0:T(2,128)}, f32[2,512]{1,0:T(2,128)S(1)}, u32[]{:S(2)}) copy-start(f32[2,512]{1,0:T(2,128)S(1)} %fusion.188) | copy-start | bytes 12292 | tf_op jit(solution)/shard_map/transpose(jvp())/while
  162.8 2.0 copy-start.21
  162.8 3.9 %copy-start.18 = (bf16[1024,2,64]{0,2,1:T(8,128)(2,1)S(1)}, bf16[1024,2,64]{0,2,1:T(8,128)(2,1)}, u32[]{:S(2)}) copy-start(bf16[1024,2,64]{0,2,1:T(8,128)(2,1)} %get-tuple-element.585) | copy-start | bytes 786436 | tf_op jit(solution)/shard_map/transpose(jvp())/while
  164.8 2.0 copy-start.2
  164.8 1.9 copy-start.13
  168.9 4.6 %copy-start.3 = (f32[2,512,1024]{2,1,0:T(8,128)S(1)}, f32[2,512,1024]{2,1,0:T(8,128)}, u32[]{:S(2)}) copy-start(f32[2,512,1024]{2,1,0:T(8,128)} %copy-done.2) | copy-start | bytes 12582916 | tf_op jit(solution)/shard_map/transpose(jvp())/while
  168.9 4.6 %copy-start.14 = (f32[2,512]{1,0:T(2,128)S(1)}, f32[2,512]{1,0:T(2,128)}, u32[]{:S(2)}) copy-start(f32[2,512]{1,0:T(2,128)} %copy-done.13) | copy-start | bytes 12292 | tf_op jit(solution)/shard_map/transpose(jvp())/while
  168.9 4.6 %copy-start.22 = (pred[2,512,1024]{2,1,0:T(32,128)(4,1)S(1)}, pred[2,512,1024]{2,1,0:T(32,128)(4,1)}, u32[]{:S(2)}) copy-start(pred[2,512,1024]{2,1,0:T(32,128)(4,1)} %copy-done.21) | copy-start | bytes 3145732 | tf_op jit(solution)/shard_map/transpose(jvp())/while
  176.7 3.7 %copy-start.12 = (bf16[1024,2,64]{0,2,1:T(8,128)(2,1)S(1)}, bf16[1024,2,64]{0,2,1:T(8,128)(2,1)}, u32[]{:S(2)}) copy-start(bf16[1024,2,64]{0,2,1:T(8,128)(2,1)} %get-tuple-element.274) | copy-start | bytes 786436
Sparse Core Ops, SparseCore 0:
  66.4 49.7 all-reduce.1
  131.3 63.3 reduce-scatter.4
  198.2 65.0 reduce-scatter.2
where the time goes:
time: 273 us; the launch traced here: 272 us
  waiting for transfers between devices  113 us (41%)
  matrix products  62 us (23%)
  other arithmetic  29 us (11%)
  blocking collectives  21.8 us (8%)
  local copies, waits for them, and re-layouts  20.8 us (8%)
  between operations  14.1 us (5%)
  starting transfers between devices  11.2 us (4%)
    reduce_scatter x1, waiting for transfers between devices, shards(): lax.psum_scatter(qkv_terms, 'dp', scatter_dimension=0, tiled=True)  57 us
    psum x1, waiting for transfers between devices, shards(): mixed = lax.psum(partial_mix.astype(jnp.bfloat16), 'mp').astype(jnp.float32)  48.4 us
    psum x1, blocking collectives, shards(): count = lax.psum(jnp.sum(masked), 'dp')  21.8 us
    dot_general x6, matrix products, one_block(): jnp.einsum('hqk,khd->qhd', probs, valued, preferred_element_type=jnp.floa...  20.7 us
    dot_general x6, matrix products, one_block(): jnp.einsum('qhd,khd->hqk', query_block, keyed, preferred_element_type=jnp...  14 us
    sub x2, matrix products, one_block(): weights = jnp.exp(scores - top)  9.01 us
    all_to_all x1, starting transfers between devices, shards(): lax.all_to_all(outgoing(noise_blocks), 'dp', split_axis=0, concat_axis=0,...  7.31 us
  transfers between devices with their start and end apart: 5, of which 4 were waited for; matrix products, arithmetic and copies ran while one was open for 22% of the time, Pallas kernels for 0%

commit v1 on v0

--- a/solution.py
+++ b/solution.py
@@ -5,6 +5,12 @@
 
 HEAD_DIM = 64
 BLOCK = 128
+
+
+def summed_here(x, axis):
+    parts = lax.all_gather(x, axis, axis=0, tiled=False)
+    total = parts.sum(axis=0)
+    return total
 
 
 def frame_table(lengths, starts, sizes, steps, rows):
@@ -131,7 +137,7 @@
     heads_out, pullback = jax.vjp(lambda a, b, c: attend(a, b, c, segment), query, keys, values)
     attended = heads_out.astype(jnp.bfloat16)
     partial_mix = jnp.dot(attended, out_proj, preferred_element_type=jnp.float32)
-    mixed = lax.psum(partial_mix.astype(jnp.bfloat16), "mp").astype(jnp.float32)
+    mixed = summed_here(partial_mix.astype(jnp.bfloat16), "mp").astype(jnp.float32)
     hidden1 = (hidden0 + mixed).astype(jnp.bfloat16)
     wide1 = lax.optimization_barrier(hidden1).astype(jnp.float32)
     rscale = lax.rsqrt(jnp.mean(wide1 * wide1, axis=1, keepdims=True) + 1e-06)

time: 273 us -> 289 us (1.059)
  other arithmetic: 29 us -> 35.6 us
  waiting for transfers between devices: 113 us -> 119 us
    all_gather x0 -> x1, waiting for transfers between devices: none -> 55.3 us  [summed_here(): parts = lax.all_gather(x, axis, axis=0, tiled=False)]
    psum x1 -> x0, waiting for transfers between devices: 48.4 us -> none  [shards(): mixed = lax.psum(partial_mix.astype(jnp.bfloat16), 'mp').astype(jnp.float32)]
    reduce_sum x0 -> x1, other arithmetic: none -> 6.5 us  [summed_here(): total = parts.sum(axis=0)]
  transfers between devices with their start and end apart: 5 -> 5, of which waited for: 4 -> 4; matrix products, arithmetic and copies ran while one was open for 22% -> 20% of each run, Pallas kernels for 0% -> 0%
where the time goes in v1:
time: 289 us; the launch traced here: 288 us
  waiting for transfers between devices  119 us (41%)
  matrix products  61.8 us (21%)
  other arithmetic  35.6 us (12%)
  local copies, waits for them, and re-layouts  23.3 us (8%)
  blocking collectives  21.9 us (8%)
  between operations  14.1 us (5%)
  starting transfers between devices  11.4 us (4%)
    reduce_scatter x1, waiting for transfers between devices, shards(): lax.psum_scatter(qkv_terms, 'dp', scatter_dimension=0, tiled=True)  56.7 us
    all_gather x1, waiting for transfers between devices, summed_here(): parts = lax.all_gather(x, axis, axis=0, tiled=False)  55.3 us
    psum x1, blocking collectives, shards(): count = lax.psum(jnp.sum(masked), 'dp')  21.9 us
    dot_general x6, matrix products, one_block(): jnp.einsum('hqk,khd->qhd', probs, valued, preferred_element_type=jnp.floa...  20.6 us
    dot_general x6, matrix products, one_block(): jnp.einsum('qhd,khd->hqk', query_block, keyed, preferred_element_type=jnp...  13.9 us
    sub x2, matrix products, one_block(): weights = jnp.exp(scores - top)  8.92 us
    all_to_all x1, starting transfers between devices, shards(): lax.all_to_all(outgoing(noise_blocks), 'dp', split_axis=0, concat_axis=0,...  7.31 us
    reduce_sum x1, other arithmetic, summed_here(): total = parts.sum(axis=0)  6.5 us
  transfers between devices with their start and end apart: 5, of which 4 were waited for; matrix products, arithmetic and copies ran while one was open for 20% of the time, Pallas kernels for 0%

profile of v1, /device:TPU:0, one launch (start us, length us, event | category | flops | bytes accessed | tf_op | source)
XLA Modules:
  0.0 287.8 jit_solution(14268232974094928721)
XLA Ops:
  8.3 1.1 fusion.60
  11.4 7.3 %all-to-all-start = ((bf16[8,2,6400]{2,1,0:T(2,128)(2,1)}), bf16[8,2,6400]{2,1,0:T(2,128)(2,1)S(1)}, u32[]{:S(2)}, u32[]{:S(2)}) async-start(bf16[8,2,6400]{2,1,0:T(2,128)(2,1)} %reshape.345), calls=%async_computation | async-start | bytes 409600 | tf_op jit(solution)/shard_map/all_to_all | solution.py:109
  21.7 1.1 fusion.61
  24.4 2.4 all-to-all-done
  26.8 3.6 %all-to-all-start.1 = ((bf16[8,2,6400]{2,1,0:T(2,128)(2,1)}), bf16[8,2,6400]{2,1,0:T(2,128)(2,1)S(1)}, u32[]{:S(2)}, u32[]{:S(2)}) async-start(bf16[8,2,6400]{2,1,0:T(2,128)(2,1)} %reshape.343), calls=%async_computation.1 | async-start | bytes 409600 | tf_op jit(solution)/shard_map/all_to_all | solution.py:110
  33.4 4.8 %all-to-all-done.1 = bf16[8,2,6400]{2,1,0:T(2,128)(2,1)S(1)} async-done(((bf16[8,2,6400]{2,1,0:T(2,128)(2,1)}), bf16[8,2,6400]{2,1,0:T(2,128)(2,1)S(1)}, u32[]{:S(2)}, u32[]{:S(2)}) %all-to-all-start.1) | async-done | bytes 204832 | tf_op jit(solution)/shard_map/all_to_all | solution.py:110
  41.4 1.3 copy-done.16
  44.0 1.2 convolution_convert_fusion.7
  46.5 17.5 %while.30 = (s32[]{:T(128)}, bf16[2,512,128]{2,1,0:T(8,128)(2,1)S(1)}, s32[2,512]{1,0:T(2,128)}, s32[1,1024]{1,0:T(1,128)S(1)}, bf16[2,512,2,64]{1,3,2,0:T(8,128...) while((s32[]{:T(128)}, bf16[2,512,128]{2,1,0:T(8,128)(2,1)S(1)}, ...), condition=%wide.region_13.14_spmd, body=%wide.region_10.13_spmd.sunk | while | flops 275252224 | bytes 11815545 | solution.py:58
  47.6 4.5 %fusion.178 = (f32[2,512]{1,0:T(2,128)S(1)}, f32[2,512,1024]{2,1,0:T(8,128)}) fusion(pred[512,1024]{1,0:T(8,128)(4,1)S(1)} %broadcast_compare_fusion.4, bf16[1024,2,64]{0,2,1:T(8,128)(2,1)S(1)} %get-tuple-element.617, bf16[2,512,2,64]{1,3,2,0:T(8,128)(2,1)} %get-tuple-element.616, s32[]{:T(128)} %get-tuple-element.604), kind=kOutput, calls=%fused_computation.176.clone.1 | convolution fusion | flops 138413056 | bytes 5116416 | tf_op jit(solution)/shard_map/jvp()/while/body/eval_jaxpr/sub | solution.py:52
  52.1 3.0 %fusion.179 = bf16[2,512,64]{1,2,0:T(8,128)(2,1)S(1)} fusion(bf16[1024,2,64]{0,2,1:T(8,128)(2,1)S(1)} %copy-done.19, f32[2,512,1024]{2,1,0:T(8,128)} %get-tuple-element.570, f32[2,512]{1,0:T(2,128)S(1)} %get-tuple-element.571), kind=kOutput, calls=%fused_computation.8.clone.1 | convolution fusion | flops 136314880 | bytes 4591616 | tf_op jit(solution)/shard_map/jvp()/while/body/eval_jaxpr/hqk,khd->qhd/dot_general | solution.py:54
  56.3 4.5 %fusion.178 = (f32[2,512]{1,0:T(2,128)S(1)}, f32[2,512,1024]{2,1,0:T(8,128)}) fusion(pred[512,1024]{1,0:T(8,128)(4,1)S(1)} %broadcast_compare_fusion.4, bf16[1024,2,64]{0,2,1:T(8,128)(2,1)S(1)} %get-tuple-element.617, bf16[2,512,2,64]{1,3,2,0:T(8,128)(2,1)} %get-tuple-element.616, s32[]{:T(128)} %get-tuple-element.604), kind=kOutput, calls=%fused_computation.176.clone.1 | convolution fusion | flops 138413056 | bytes 5116416 | tf_op jit(solution)/shard_map/jvp()/while/body/eval_jaxpr/sub | solution.py:52
  60.8 3.0 %fusion.179 = bf16[2,512,64]{1,2,0:T(8,128)(2,1)S(1)} fusion(bf16[1024,2,64]{0,2,1:T(8,128)(2,1)S(1)} %copy-done.19, f32[2,512,1024]{2,1,0:T(8,128)} %get-tuple-element.570, f32[2,512]{1,0:T(2,128)S(1)} %get-tuple-element.571), kind=kOutput, calls=%fused_computation.8.clone.1 | convolution fusion | flops 136314880 | bytes 4591616 | tf_op jit(solution)/shard_map/jvp()/while/body/eval_jaxpr/hqk,khd->qhd/dot_general | solution.py:54
  64.0 2.0 convolution_convert_fusion.5
  67.6 55.3 %all-gather.3.cloned.1.call-done = bf16[4096,1024]{1,0:T(8,128)(2,1)} async-done(((bf16[1024,1024]{1,0:T(8,128)(2,1)}), bf16[4096,1024]{1,0:T(8,128)(2,1)}) %all-gather.3.cloned.1.call-update) | async-done | bytes 8388624 | tf_op jit(solution)/shard_map/all_gather | solution.py:11
  122.8 6.5 %reduce_sum.208 = bf16[1024,1024]{1,0:T(8,128)(2,1)S(1)} reduce(bf16[4,1024,1024]{2,1,0:T(8,128)(2,1)} %bitcast.162, bf16[]{:T(256)} %constant.183.clone.1), dimensions={0}, to_apply=%region_14.15 | reduce | flops 3145728 | bytes 10485762 | tf_op jit(solution)/shard_map/reduce_sum | solution.py:12
  129.3 2.6 copy.51
  131.9 3.6 %add_convert_fusion = bf16[1024,1024]{0,1:T(8,128)(2,1)S(1)} fusion(f32[1024,1024]{0,1:T(8,128)} %copy-done.4, bf16[1024,1024]{0,1:T(8,128)(2,1)} %copy.51), kind=kLoop, calls=%fused_computation.88 | loop fusion | flops 3145728 | bytes 8388608 | tf_op jit(solution)/shard_map/convert_element_type | solution.py:141
  136.1 4.7 %fusion.66 = (f32[1024]{0:T(1024)S(1)}, f32[1024,1024]{0,1:T(8,128)}) fusion(bf16[1024,1024]{0,1:T(8,128)(2,1)S(1)} %add_convert_fusion, f32[1024]{0:T(1024)S(1)} %convert_element_type.202, f32[1024]{0:T(1024)S(1)} %add_rsqrt_fusion, bf16[1024,100]{0,1:T(8,128)(2,1)} %param.29, f32[1024,100]{0,1:T(8,128)} %copy.52, f32[1024,100]{0,1:T(8,128)S(1)} %copy.53, ...), kind=kOutput, calls=%fused_computation.83 | convolution fusion | flops 429276160 | bytes 7331840 | tf_op jit(solution)/shard_map/dot_general | solution.py:150
  140.8 3.7 %fusion.69 = bf16[1024,1024]{0,1:T(8,128)(2,1)S(1)} fusion(bf16[1024,1024]{0,1:T(8,128)(2,1)} %copy-done.7, f32[1024,1024]{0,1:T(8,128)} %get-tuple-element.459, f32[1024]{0:T(1024)S(1)} %broadcast_multiply_fusion, f32[1024]{0:T(1024)S(1)} %convert_element_type.202, f32[1024]{0:T(1024)S(1)} %add_rsqrt_fusion), kind=kLoop, calls=%fused_computation.86 | loop fusion | flops 7340032 | bytes 8400896 | tf_op jit(solution)/shard_map/convert_element_type | solution.py:154
  144.5 1.6 fusion.126
  148.0 44.7 %while.31 = (s32[]{:T(128)}, bf16[1024,2,64]{0,2,1:T(8,128)(2,1)}, bf16[1024,2,64]{0,2,1:T(8,128)(2,1)}, bf16[2,512,2,64]{1,3,2,0:T(8,128)(2,1)}, bf16[2,512,2,6...) while((s32[]{:T(128)}, bf16[1024,2,64]{0,2,1:T(8,128)(2,1)}, ...), condition=%wide.region_23.24_spmd.clone, body=%wide.region_17.23_spmd.clone.sunk | while | flops 712179712 | bytes 109349352 | solution.py:58
  148.1 1.0 dynamic-slice_bitcast_fusion.2
  149.8 1.0 broadcast_compare_fusion.5
  150.9 2.1 fusion.187
  153.0 1.2 fusion.188
  154.2 2.8 convert_reduce_fusion.5
  157.0 1.9 fusion.189
  159.0 1.9 copy-done.2
  160.9 2.2 fusion.192
  163.1 4.5 %fusion.191 = bf16[1024,2,64]{0,2,1:T(8,128)(2,1)} fusion(bf16[2,64,512]{2,1,0:T(8,128)(2,1)S(1)} %bitcast.165, f32[2,512]{1,0:T(2,128)} %copy-done.9, f32[2,512,1024]{2,1,0:T(8,128)} %copy-done.1, f32[2,512]{1,0:T(2,128)} %copy-done.11, pred[512,1024]{1,0:T(8,128)(4,1)S(1)} %broadcast_compare_fusion.5, ...), kind=kOutput, calls=%fused_computation.52.clone.1 | convolution fusion | flops 139722752 | bytes 5382145 | tf_op jit(solution)/shard_map/transpose(jvp())/while/body/eval_jaxpr/checkpoint/hqk,khd->qhd/dot_general | solution.py:54
  167.6 2.3 fusion.190
  171.6 1.0 broadcast_compare_fusion.5
  172.7 2.1 fusion.187
  174.8 1.2 fusion.188
  176.0 2.8 convert_reduce_fusion.5
  178.8 1.9 fusion.189
  180.8 1.9 copy-done.2
  182.7 2.1 fusion.192
  184.9 4.5 %fusion.191 = bf16[1024,2,64]{0,2,1:T(8,128)(2,1)} fusion(bf16[2,64,512]{2,1,0:T(8,128)(2,1)S(1)} %bitcast.165, f32[2,512]{1,0:T(2,128)} %copy-done.9, f32[2,512,1024]{2,1,0:T(8,128)} %copy-done.1, f32[2,512]{1,0:T(2,128)} %copy-done.11, pred[512,1024]{1,0:T(8,128)(4,1)S(1)} %broadcast_compare_fusion.5, ...), kind=kOutput, calls=%fused_computation.52.clone.1 | convolution fusion | flops 139722752 | bytes 5382145 | tf_op jit(solution)/shard_map/transpose(jvp())/while/body/eval_jaxpr/checkpoint/hqk,khd->qhd/dot_general | solution.py:54
  189.4 3.2 %fusion.190 = bf16[1024,2,64]{0,2,1:T(8,128)(2,1)} fusion(bf16[512,2,64]{0,2,1:T(8,128)(2,1)S(1)} %dynamic-slice_bitcast_fusion.2, f32[2,512,1024]{2,1,0:T(8,128)S(1)} %copy-done.3, pred[2,512,1024]{2,1,0:T(32,128)(4,1)S(1)} %copy-done.22, f32[2,512]{1,0:T(2,128)S(1)} %copy-done.14, pred[512,1024]{1,0:T(8,128)(4,1)S(1)} %broadcast_compare_fusion.5, ...), kind=kOutput, calls=%fused_computation.53.clone.1 | convolution fusion | flops 138805248 | bytes 6426625 | tf_op jit(solution)/shard_map/transpose(jvp())/while/body/eval_jaxpr/checkpoint/qhd,khd->hqk/dot_general | solution.py:47
  192.6 1.3 copy.56
  194.6 1.7 convolution_bitcast_fusion.1
  197.0 1.3 pad_maximum_fusion
  198.3 21.9 %psum.7 = f32[]{:T(128)} all-reduce(f32[]{:T(128)} %get-tuple-element.442), channel_id=1, replica_groups=mesh['dp'=8,'mp'=4] {'dp'}, use_global_device_ids=true, to_apply=%region_26.27 | all-reduce | flops 1 | bytes 8 | tf_op jit(solution)/shard_map/psum | solution.py:148
  220.2 2.1 broadcast_divide_fusion.1
  222.3 56.7 %reduce-scatter.3.cloned.1.call-done = f32[128,3,128]{2,0,1:T(8,128)} async-done(((f32[1024,3,128]{2,0,1:T(8,128)}), f32[128,3,128]{2,0,1:T(8,128)}) %reduce-scatter.3.cloned.1.call-update) | async-done | bytes 196624 | tf_op jit(solution)/shard_map/reduce_scatter | solution.py:167
  279.0 2.2 broadcast_divide_fusion
  (146 shorter events, 26.6 us)
Async XLA Ops:
  7.2 32.9 %copy-start = (bf16[200,1024]{1,0:T(8,128)(2,1)S(1)}, bf16[200,1024]{1,0:T(8,128)(2,1)}, u32[]{:S(2)}) copy-start(bf16[200,1024]{1,0:T(8,128)(2,1)} %param.24) | copy-start | bytes 1228804
  11.4 15.4 %all-to-all-start = ((bf16[8,2,6400]{2,1,0:T(2,128)(2,1)}), bf16[8,2,6400]{2,1,0:T(2,128)(2,1)S(1)}, u32[]{:S(2)}, u32[]{:S(2)}) async-start(bf16[8,2,6400]{2,1,0:T(2,128)(2,1)} %reshape.345), calls=%async_computation | async-start | bytes 409600 | tf_op jit(solution)/shard_map/all_to_all | solution.py:109
  26.8 11.4 %all-to-all-start.1 = ((bf16[8,2,6400]{2,1,0:T(2,128)(2,1)}), bf16[8,2,6400]{2,1,0:T(2,128)(2,1)S(1)}, u32[]{:S(2)}, u32[]{:S(2)}) async-start(bf16[8,2,6400]{2,1,0:T(2,128)(2,1)} %reshape.343), calls=%async_computation.1 | async-start | bytes 409600 | tf_op jit(solution)/shard_map/all_to_all | solution.py:110
  30.4 92.5 %all-gather.3.cloned.1.call-start = ((), (), s32[]{:S(2)}) async-start(), calls=%async_computation.6 | async-start | bytes 10485760 | tf_op jit(solution)/shard_map/all_gather | solution.py:11
  40.9 2.5 copy-start.4
  41.0 1.7 copy-start.16
  42.7 1.4 copy-start.5
  46.5 17.5 %copy-start.8 = (bf16[128,1024]{1,0:T(8,128)(2,1)S(1)}, bf16[128,1024]{1,0:T(8,128)(2,1)}, u32[]{:S(2)}) copy-start(bf16[128,1024]{1,0:T(8,128)(2,1)} %param.27) | copy-start | bytes 786436
  47.2 4.8 %copy-start.19 = (bf16[1024,2,64]{0,2,1:T(8,128)(2,1)S(1)}, bf16[1024,2,64]{0,2,1:T(8,128)(2,1)}, u32[]{:S(2)}) copy-start(bf16[1024,2,64]{0,2,1:T(8,128)(2,1)} %get-tuple-element.618) | copy-start | bytes 786436 | tf_op jit(solution)/shard_map/jvp()/while
  56.0 4.8 %copy-start.19 = (bf16[1024,2,64]{0,2,1:T(8,128)(2,1)S(1)}, bf16[1024,2,64]{0,2,1:T(8,128)(2,1)}, u32[]{:S(2)}) copy-start(bf16[1024,2,64]{0,2,1:T(8,128)(2,1)} %get-tuple-element.618) | copy-start | bytes 786436 | tf_op jit(solution)/shard_map/jvp()/while
  64.0 2.3 copy-start.17
  64.0 58.8 %copy-start.10 = (s32[1,1024]{1,0:T(1,128)}, s32[1,1024]{1,0:T(1,128)S(1)}, u32[]{:S(2)}) copy-start(s32[1,1024]{1,0:T(1,128)S(1)} %get-tuple-element.668) | copy-start | bytes 12292
  64.0 2.3 copy-start.15
  66.1 154.2 %reduce-scatter.5.cloned.1.call-start = ((), (), s32[]{:S(2)}) async-start(), calls=%async_computation.5 | async-start | bytes 589824 | tf_op jit(solution)/shard_map/reduce_scatter | solution.py:168
  135.6 5.2 %copy-start.7 = (bf16[1024,1024]{0,1:T(8,128)(2,1)}, bf16[1024,1024]{0,1:T(8,128)(2,1)S(1)}, u32[]{:S(2)}) copy-start(bf16[1024,1024]{0,1:T(8,128)(2,1)S(1)} %add_convert_fusion) | copy-start | bytes 6291460
  147.0 132.0 %reduce-scatter.3.cloned.1.call-start = ((), (), s32[]{:S(2)}) async-start(), calls=%async_computation.4 | async-start | bytes 1769472 | tf_op jit(solution)/shard_map/reduce_scatter | solution.py:167
  148.0 46.0 %copy-start.6 = (bf16[1024,1024]{0,1:T(8,128)(2,1)S(1)}, bf16[1024,1024]{0,1:T(8,128)(2,1)}, u32[]{:S(2)}) copy-start(bf16[1024,1024]{0,1:T(8,128)(2,1)} %copy-done.5) | copy-start | bytes 6291460
  150.9 3.3 %copy-start.20 = (bf16[1024,2,64]{0,2,1:T(8,128)(2,1)S(1)}, bf16[1024,2,64]{0,2,1:T(8,128)(2,1)}, u32[]{:S(2)}) copy-start(bf16[1024,2,64]{0,2,1:T(8,128)(2,1)} %get-tuple-element.589) | copy-start | bytes 786436 | tf_op jit(solution)/shard_map/transpose(jvp())/while
  153.0 4.0 %copy-start.1 = (f32[2,512,1024]{2,1,0:T(8,128)}, f32[2,512,1024]{2,1,0:T(8,128)S(1)}, u32[]{:S(2)}) copy-start(f32[2,512,1024]{2,1,0:T(8,128)S(1)} %get-tuple-element.587) | copy-start | bytes 12582916 | tf_op jit(solution)/shard_map/transpose(jvp())/while
  153.0 4.0 %copy-start.11 = (f32[2,512]{1,0:T(2,128)}, f32[2,512]{1,0:T(2,128)S(1)}, u32[]{:S(2)}) copy-start(f32[2,512]{1,0:T(2,128)S(1)} %get-tuple-element.586) | copy-start | bytes 12292 | tf_op jit(solution)/shard_map/transpose(jvp())/while
  154.2 2.9 copy-start.9
  157.0 2.0 copy-start.21
  157.0 3.9 %copy-start.18 = (bf16[1024,2,64]{0,2,1:T(8,128)(2,1)S(1)}, bf16[1024,2,64]{0,2,1:T(8,128)(2,1)}, u32[]{:S(2)}) copy-start(bf16[1024,2,64]{0,2,1:T(8,128)(2,1)} %get-tuple-element.585) | copy-start | bytes 786436 | tf_op jit(solution)/shard_map/transpose(jvp())/while
  158.9 2.0 copy-start.2
  159.0 1.9 copy-start.13
  163.1 4.5 %copy-start.3 = (f32[2,512,1024]{2,1,0:T(8,128)S(1)}, f32[2,512,1024]{2,1,0:T(8,128)}, u32[]{:S(2)}) copy-start(f32[2,512,1024]{2,1,0:T(8,128)} %copy-done.2) | copy-start | bytes 12582916 | tf_op jit(solution)/shard_map/transpose(jvp())/while
  163.1 4.5 %copy-start.14 = (f32[2,512]{1,0:T(2,128)S(1)}, f32[2,512]{1,0:T(2,128)}, u32[]{:S(2)}) copy-start(f32[2,512]{1,0:T(2,128)} %copy-done.13) | copy-start | bytes 12292 | tf_op jit(solution)/shard_map/transpose(jvp())/while
  163.1 4.5 %copy-start.22 = (pred[2,512,1024]{2,1,0:T(32,128)(4,1)S(1)}, pred[2,512,1024]{2,1,0:T(32,128)(4,1)}, u32[]{:S(2)}) copy-start(pred[2,512,1024]{2,1,0:T(32,128)(4,1)} %copy-done.21) | copy-start | bytes 3145732 | tf_op jit(solution)/shard_map/transpose(jvp())/while
  172.7 3.3 %copy-start.20 = (bf16[1024,2,64]{0,2,1:T(8,128)(2,1)S(1)}, bf16[1024,2,64]{0,2,1:T(8,128)(2,1)}, u32[]{:S(2)}) copy-start(bf16[1024,2,64]{0,2,1:T(8,128)(2,1)} %get-tuple-element.589) | copy-start | bytes 786436 | tf_op jit(solution)/shard_map/transpose(jvp())/while
  174.8 4.0 %copy-start.1 = (f32[2,512,1024]{2,1,0:T(8,128)}, f32[2,512,1024]{2,1,0:T(8,128)S(1)}, u32[]{:S(2)}) copy-start(f32[2,512,1024]{2,1,0:T(8,128)S(1)} %get-tuple-element.587) | copy-start | bytes 12582916 | tf_op jit(solution)/shard_map/transpose(jvp())/while
  174.8 4.0 %copy-start.11 = (f32[2,512]{1,0:T(2,128)}, f32[2,512]{1,0:T(2,128)S(1)}, u32[]{:S(2)}) copy-start(f32[2,512]{1,0:T(2,128)S(1)} %get-tuple-element.586) | copy-start | bytes 12292 | tf_op jit(solution)/shard_map/transpose(jvp())/while
  175.9 2.9 copy-start.9
  178.8 2.0 copy-start.21
  178.8 3.9 %copy-start.18 = (bf16[1024,2,64]{0,2,1:T(8,128)(2,1)S(1)}, bf16[1024,2,64]{0,2,1:T(8,128)(2,1)}, u32[]{:S(2)}) copy-start(bf16[1024,2,64]{0,2,1:T(8,128)(2,1)} %get-tuple-element.585) | copy-start | bytes 786436 | tf_op jit(solution)/shard_map/transpose(jvp())/while
  180.7 2.0 copy-start.2
  180.8 1.9 copy-start.13
  184.9 4.5 %copy-start.3 = (f32[2,512,1024]{2,1,0:T(8,128)S(1)}, f32[2,512,1024]{2,1,0:T(8,128)}, u32[]{:S(2)}) copy-start(f32[2,512,1024]{2,1,0:T(8,128)} %copy-done.2) | copy-start | bytes 12582916 | tf_op jit(solution)/shard_map/transpose(jvp())/while
  184.9 4.5 %copy-start.14 = (f32[2,512]{1,0:T(2,128)S(1)}, f32[2,512]{1,0:T(2,128)}, u32[]{:S(2)}) copy-start(f32[2,512]{1,0:T(2,128)} %copy-done.13) | copy-start | bytes 12292 | tf_op jit(solution)/shard_map/transpose(jvp())/while
  184.9 4.5 %copy-start.22 = (pred[2,512,1024]{2,1,0:T(32,128)(4,1)S(1)}, pred[2,512,1024]{2,1,0:T(32,128)(4,1)}, u32[]{:S(2)}) copy-start(pred[2,512,1024]{2,1,0:T(32,128)(4,1)} %copy-done.21) | copy-start | bytes 3145732 | tf_op jit(solution)/shard_map/transpose(jvp())/while
  192.6 3.7 %copy-start.12 = (bf16[1024,2,64]{0,2,1:T(8,128)(2,1)S(1)}, bf16[1024,2,64]{0,2,1:T(8,128)(2,1)}, u32[]{:S(2)}) copy-start(bf16[1024,2,64]{0,2,1:T(8,128)(2,1)} %get-tuple-element.274) | copy-start | bytes 786436
Sparse Core Ops, SparseCore 0:
  66.2 56.5 all-gather.2
  147.1 63.2 reduce-scatter.4
  213.8 65.1 reduce-scatter.2
